TPU v7x, 32 devices: a whole 2x2x4 slice. The times are simulated.
32 devices in a mesh: dp: 8 (over y, x, core), expert: 4 (over z).
Axes of the slice: x: 2, y: 2, z: 4, core: 2. Of those that a mesh axis runs over, the one named last changes fastest.
Arguments:
- hidden_states: bfloat16 [4, 8192, 4096], P(None, ('dp', 'expert')), may hold values from -8 to 8
- router_weight: bfloat16 [4, 8, 4096], replicated, may hold values from -0.125 to 0.125
- expert_ids: int32 [4, 8192, 2], P(None, ('dp', 'expert')), may hold values from 0 to 7, as said below
Outputs:
- router_grad: float32 [4, 8, 4096], P(None, None, 'dp')
- losses: float32 [4, 2], replicated
Inputs may be any that keep to these rules, and one draw needn't show every extreme that they name: `expert_ids`: each token names 2 different experts in each layer.
All inputs are finite; a program needn't handle non-finite values.
Results may differ from a plain program's by a relative error of at most 0.0018.
Values sent between devices are 32-bit elements; how exact they have to be, the bound alone decides.
A program may use at most 64 MiB of HBM per device.

v0:
```python
import jax
import jax.numpy as jnp
from jax import lax
from jax.sharding import PartitionSpec as P

balance_coef = 0.02
zloss_coef = 0.001


def local_counts(chosen, experts):
    labels = jnp.arange(experts, dtype=jnp.int32)[:, None]
    counts = jnp.zeros((experts,), jnp.float32)
    for slot in range(chosen.shape[1]):
        counts = counts + jnp.sum((chosen[:, slot][None, :] == labels).astype(jnp.float32), axis=1)
    return counts


def on_device(hidden_states, router_weight, expert_ids):
    layers = hidden_states.shape[0]
    rows = hidden_states.shape[1]
    experts = router_weight.shape[1]
    picks = expert_ids.shape[2]
    tokens_all = rows * lax.axis_size("dp") * lax.axis_size("expert")
    terms = []
    count_list = []
    prob_sums = []
    square_sums = []
    for layer in range(layers):
        states = hidden_states[layer]
        logits = lax.dot_general(
            router_weight[layer],
            states,
            (((1,), (1,)), ((), ())),
            preferred_element_type=jnp.float32,
        )
        expo = jnp.exp(logits)
        total = jnp.sum(expo, axis=0)
        probs = expo / total[None, :]
        lse = jnp.log(total)
        prob_sums.append(jnp.sum(probs, axis=1))
        square_sums.append(jnp.sum(lse * lse))
        counts = lax.psum(local_counts(expert_ids[layer], experts), ("dp", "expert"))
        count_list.append(counts)
        share = counts / (tokens_all * picks)
        pull = balance_coef * experts * share
        mixed = jnp.sum(probs * pull[:, None], axis=0)
        dlogits = probs * (pull[:, None] - mixed[None, :]) + 2.0 * zloss_coef * lse[None, :] * probs
        dlogits = dlogits.astype(jnp.bfloat16)
        term = jnp.dot(dlogits, states, preferred_element_type=jnp.float32)
        terms.append(term)
    columns = lax.psum_scatter(jnp.stack(terms), "dp", scatter_dimension=2, tiled=True)
    router_grad = lax.psum(columns, "expert")
    prob_total, square_total = lax.psum(
        (jnp.stack(prob_sums), jnp.stack(square_sums)), ("dp", "expert")
    )
    share_table = jnp.stack(count_list) / (tokens_all * picks)
    balance = experts * jnp.sum(share_table * prob_total / tokens_all, axis=1)
    zloss = square_total / tokens_all
    return (router_grad, jnp.stack([balance, zloss], axis=-1))


def solution(mesh):
    in_specs = (P(None, ("dp", "expert"), None), P(), P(None, ("dp", "expert"), None))
    out_specs = (P(None, None, "dp"), P())
    return jax.shard_map(
        on_device, mesh=mesh, in_specs=in_specs, out_specs=out_specs, check_vma=False
    )
```

profile of v0, /device:TPU:0, one launch (start us, length us, event | category | flops | bytes accessed | tf_op | source)
XLA Modules:
  0.0 158.2 jit_solution(140643967143512886)
XLA Ops:
  7.2 2.3 %fusion.65 = (f32[256]{0:T(256)S(1)}, f32[8,256]{1,0:T(8,128)S(1)}) fusion(bf16[4,256,4096]{2,1,0:T(8,128)(2,1)} %param.3, bf16[4,8,4096]{2,1,0:T(8,128)(2,1)} %param.4), kind=kOutput, calls=%fused_computation.112 | convolution fusion | flops 16779008 | bytes 2171904 | tf_op jit(solution)/shard_map/dot_general | solution.py:30
  9.5 2.3 %fusion.66 = (f32[256]{0:T(256)S(1)}, f32[8,256]{1,0:T(8,128)S(1)}) fusion(bf16[4,256,4096]{2,1,0:T(8,128)(2,1)} %param.3, bf16[4,8,4096]{2,1,0:T(8,128)(2,1)} %param.4), kind=kOutput, calls=%fused_computation.113 | convolution fusion | flops 16779008 | bytes 2171904 | tf_op jit(solution)/shard_map/dot_general | solution.py:30
  11.8 2.3 %fusion.63 = (f32[256]{0:T(256)S(1)}, f32[8,256]{1,0:T(8,128)S(1)}) fusion(bf16[4,256,4096]{2,1,0:T(8,128)(2,1)} %param.3, bf16[4,8,4096]{2,1,0:T(8,128)(2,1)} %param.4), kind=kOutput, calls=%fused_computation.110 | convolution fusion | flops 16779008 | bytes 2171904 | tf_op jit(solution)/shard_map/dot_general | solution.py:30
  14.1 0.7 slice_bitcast_fusion.3
  14.9 0.1 convert_reduce_fusion.6
  15.0 0.1 convert_reduce_fusion.7
  15.1 0.1 convert_reduce_fusion.4
  15.2 0.1 convert_reduce_fusion.5
  15.4 0.1 convert_reduce_fusion
  15.5 0.1 convert_reduce_fusion.1
  15.6 0.1 convert_reduce_fusion.2
  15.7 0.1 convert_reduce_fusion.3
  15.9 2.3 %fusion.64 = (f32[256]{0:T(256)S(1)}, f32[8,256]{1,0:T(8,128)S(1)}) fusion(bf16[4,256,4096]{2,1,0:T(8,128)(2,1)} %param.3, bf16[4,8,4096]{2,1,0:T(8,128)(2,1)} %param.4), kind=kOutput, calls=%fused_computation.111 | convolution fusion | flops 16779008 | bytes 2171904 | tf_op jit(solution)/shard_map/dot_general | solution.py:30
  18.2 42.0 %all-reduce.1 = (f32[8]{0:T(128)S(1)}, f32[8]{0:T(128)S(1)}, f32[8]{0:T(128)S(1)}, f32[8]{0:T(128)S(1)}) all-reduce(f32[8]{0:T(128)S(1)} %add.46, f32[8]{0:T(128)S(1)} %add.44, f32[8]{0:T(128)S(1)} %add.42, f32[8]{0:T(128)S(1)} %add.40), channel_id=1, replica_groups=mesh['dp'=8,'expert'=4] {'dp','expert'}, use_global_device_ids=true, to_apply=%region_18.0 | all-reduce | flops 32 | bytes 256 | tf_op jit(solution)/shard_map/psum | solution.py:42
  60.2 0.6 multiply_reduce_fusion.6
  60.8 0.7 multiply_reduce_fusion.7
  61.5 0.6 multiply_reduce_fusion.4
  62.1 0.6 multiply_reduce_fusion.5
  62.7 0.2 fusion.55
  62.9 2.0 %convolution_bitcast_fusion.3 = f32[1,8,4096]{2,1,0:T(8,128)S(1)} fusion(bf16[4,256,4096]{2,1,0:T(8,128)(2,1)} %param.3, f32[256]{0:T(256)S(1)} %get-tuple-element.29, f32[256]{0:T(256)S(1)} %get-tuple-element.3, f32[8]{0:T(128)S(1)} %broadcast_multiply_fusion.3, f32[8,256]{1,0:T(8,128)S(1)} %get-tuple-element.43, f32[256]{0:T(256)S(1)} %get-tuple-element.42), kind=kOutput, calls=%fused_computation.3 | convolution fusion | flops 16787456 | bytes 2239520 | tf_op jit(solution)/shard_map/dot_general | solution.py:49
  64.9 2.0 %convolution_bitcast_fusion.2 = f32[1,8,4096]{2,1,0:T(8,128)S(1)} fusion(bf16[4,256,4096]{2,1,0:T(8,128)(2,1)} %param.3, f32[256]{0:T(256)S(1)} %get-tuple-element.31, f32[256]{0:T(256)S(1)} %get-tuple-element.44, f32[8]{0:T(128)S(1)} %broadcast_multiply_fusion.2, f32[8,256]{1,0:T(8,128)S(1)} %get-tuple-element.41, f32[256]{0:T(256)S(1)} %get-tuple-element.40), kind=kOutput, calls=%fused_computation.2 | convolution fusion | flops 16787456 | bytes 2239520 | tf_op jit(solution)/shard_map/dot_general | solution.py:49
  66.9 0.2 fusion.57
  67.1 2.0 %convolution_bitcast_fusion.1 = f32[1,8,4096]{2,1,0:T(8,128)S(1)} fusion(bf16[4,256,4096]{2,1,0:T(8,128)(2,1)} %param.3, f32[256]{0:T(256)S(1)} %get-tuple-element.33, f32[256]{0:T(256)S(1)} %get-tuple-element.7, f32[8]{0:T(128)S(1)} %broadcast_multiply_fusion.1, f32[8,256]{1,0:T(8,128)S(1)} %get-tuple-element.39, f32[256]{0:T(256)S(1)} %get-tuple-element.38), kind=kOutput, calls=%fused_computation.1 | convolution fusion | flops 16787456 | bytes 2239520 | tf_op jit(solution)/shard_map/dot_general | solution.py:49
  69.1 2.0 %convolution_bitcast_fusion = f32[1,8,4096]{2,1,0:T(8,128)S(1)} fusion(bf16[4,256,4096]{2,1,0:T(8,128)(2,1)} %param.3, f32[256]{0:T(256)S(1)} %get-tuple-element.35, f32[256]{0:T(256)S(1)} %get-tuple-element.46, f32[8]{0:T(128)S(1)} %broadcast_multiply_fusion, f32[8,256]{1,0:T(8,128)S(1)} %get-tuple-element.37, f32[256]{0:T(256)S(1)} %get-tuple-element.36), kind=kOutput, calls=%fused_computation | convolution fusion | flops 16787456 | bytes 2239520 | tf_op jit(solution)/shard_map/dot_general | solution.py:49
  71.1 0.8 pad_maximum_fusion
  71.9 0.0 all-reduce.4.cloned.1.call-start
  72.0 2.6 %pad_maximum_fusion.3 = f32[4]{0:T(128)S(1)} fusion(f32[1]{0:T(128)} %bitcast.36, f32[1]{0:T(128)} %bitcast.35, f32[1]{0:T(128)} %bitcast.34, f32[1]{0:T(128)} %bitcast.33), kind=kLoop, calls=%fused_computation.95 | loop fusion | flops 12 | bytes 32 | tf_op jit(solution)/shard_map/stack | solution.py:54
  74.6 40.0 %all-reduce = (f32[4]{0:T(128)S(1)}, f32[4,8]{1,0:T(4,128)S(1)}) all-reduce(f32[4]{0:T(128)S(1)} %pad_maximum_fusion.3, f32[4,8]{1,0:T(4,128)S(1)} %pad_maximum_fusion.1), channel_id=1, replica_groups=mesh['dp'=8,'expert'=4] {'dp','expert'}, use_global_device_ids=true, to_apply=%region_32.0 | all-reduce | flops 36 | bytes 288 | tf_op jit(solution)/shard_map/psum | solution.py:53
  114.7 0.1 fusion.54
  114.8 0.6 pad_maximum_fusion.2
  115.4 34.5 %all-reduce.4.cloned.1.call-done = f32[4,8,512]{2,1,0:T(8,128)} async-done(((f32[4,8,512]{2,1,0:T(8,128)}), f32[4,8,512]{2,1,0:T(8,128)}) %all-reduce.4.cloned.1.call-update) | async-done | bytes 65552 | tf_op jit(solution)/shard_map/psum | solution.py:52
  149.9 1.5 copy.6
  (19 shorter events, 0.2 us)
Async XLA Ops:
  7.2 107.6 %reduce-scatter.2.cloned.1.call-start = ((), (), s32[]{:S(2)}) async-start(), calls=%async_computation.1 | async-start | bytes 589824 | tf_op jit(solution)/shard_map/reduce_scatter | solution.py:51
  71.9 78.0 %all-reduce.4.cloned.1.call-start = ((), (), s32[]{:S(2)}) async-start(), calls=%async_computation.2 | async-start | bytes 131072 | tf_op jit(solution)/shard_map/psum | solution.py:52
Sparse Core Ops, SparseCore 0:
  72.1 33.9 reduce-scatter.1
  115.0 34.9 all-reduce.3
where the time goes:
time: 159 us; the launch traced here: 158 us
  blocking collectives  82.1 us (52%)
  waiting for transfers between devices  34.6 us (22%)
  matrix products  17.3 us (11%)
  between operations  14.2 us (9%)
  other arithmetic  7.88 us (5%)
  local copies, waits for them, and re-layouts  2.23 us (1%)
    psum x1, blocking collectives, on_device(): lax.psum(local_counts(expert_ids[layer], experts), ('dp', 'expert'))  42 us
    psum x1, blocking collectives, on_device(): lax.psum((jnp.stack(prob_sums), jnp.stack(square_sums)), ('dp', 'expert'))  40 us
    psum x1, waiting for transfers between devices, on_device(): router_grad = lax.psum(columns, 'expert')  34.5 us
    dot_general x4, matrix products, on_device(): lax.dot_general(router_weight[layer], states, (((1,), (1,)), ((), ())), p...  9.21 us
    dot_general x4, matrix products, on_device(): term = jnp.dot(dlogits, states, preferred_element_type=jnp.float32)  8.06 us
  transfers between devices with their start and end apart: 2, of which 1 were waited for; matrix products, arithmetic and copies ran while one was open for 2% of the time, Pallas kernels for 0%

commit v1 on v0

--- a/solution.py
+++ b/solution.py
@@ -49,7 +49,11 @@
         term = jnp.dot(dlogits, states, preferred_element_type=jnp.float32)
         terms.append(term)
     columns = lax.psum_scatter(jnp.stack(terms), "dp", scatter_dimension=2, tiled=True)
-    router_grad = lax.psum(columns, "expert")
+    router_grad = columns
+    for hop in (1, 2):
+        router_grad = router_grad + lax.ppermute(
+            router_grad, "expert", [(dev, dev ^ hop) for dev in range(4)]
+        )
     prob_total, square_total = lax.psum(
         (jnp.stack(prob_sums), jnp.stack(square_sums)), ("dp", "expert")
     )

time: 159 us -> 134 us (0.84)
  waiting for transfers between devices: 34.6 us -> 8.12 us
  starting transfers between devices: 0.08 us -> 1.78 us
    psum x1 -> x0, waiting for transfers between devices: 34.5 us -> none  [on_device(): router_grad = lax.psum(columns, 'expert')]
    ppermute x0 -> x2, waiting for transfers between devices: none -> 8.08 us  [on_device(): lax.ppermute(router_grad, 'expert', [(dev, dev ^ hop) for dev in range(4)])]
    ppermute x0 -> x2, starting transfers between devices: none -> 1.74 us  [on_device(): lax.ppermute(router_grad, 'expert', [(dev, dev ^ hop) for dev in range(4)])]
  transfers between devices with their start and end apart: 2 -> 3, of which waited for: 1 -> 2; matrix products, arithmetic and copies ran while one was open for 2% -> 2% of each run, Pallas kernels for 0% -> 0%
where the time goes in v1:
time: 134 us; the launch traced here: 133 us
  blocking collectives  82.1 us (61%)
  matrix products  17.3 us (13%)
  between operations  14.1 us (11%)
  other arithmetic  9.37 us (7%)
  waiting for transfers between devices  8.12 us (6%)
  starting transfers between devices  1.78 us (1%)
    psum x1, blocking collectives, on_device(): lax.psum(local_counts(expert_ids[layer], experts), ('dp', 'expert'))  42 us
    psum x1, blocking collectives, on_device(): lax.psum((jnp.stack(prob_sums), jnp.stack(square_sums)), ('dp', 'expert'))  40.1 us
    dot_general x4, matrix products, on_device(): lax.dot_general(router_weight[layer], states, (((1,), (1,)), ((), ())), p...  9.21 us
    ppermute x2, waiting for transfers between devices, on_device(): lax.ppermute(router_grad, 'expert', [(dev, dev ^ hop) for dev in range(4)])  8.08 us
    dot_general x4, matrix products, on_device(): term = jnp.dot(dlogits, states, preferred_element_type=jnp.float32)  8.06 us
  transfers between devices with their start and end apart: 3, of which 2 were waited for; matrix products, arithmetic and copies ran while one was open for 2% of the time, Pallas kernels for 0%

profile of v1, /device:TPU:0, one launch (start us, length us, event | category | flops | bytes accessed | tf_op | source)
XLA Modules:
  0.0 133.5 jit_solution(6611453607115994825)
XLA Ops:
  7.2 2.3 %fusion.65 = (f32[256]{0:T(256)S(1)}, f32[8,256]{1,0:T(8,128)S(1)}) fusion(bf16[4,256,4096]{2,1,0:T(8,128)(2,1)} %param.3, bf16[4,8,4096]{2,1,0:T(8,128)(2,1)} %param.4), kind=kOutput, calls=%fused_computation.112 | convolution fusion | flops 16779008 | bytes 2171904 | tf_op jit(solution)/shard_map/dot_general | solution.py:30
  9.5 2.3 %fusion.66 = (f32[256]{0:T(256)S(1)}, f32[8,256]{1,0:T(8,128)S(1)}) fusion(bf16[4,256,4096]{2,1,0:T(8,128)(2,1)} %param.3, bf16[4,8,4096]{2,1,0:T(8,128)(2,1)} %param.4), kind=kOutput, calls=%fused_computation.113 | convolution fusion | flops 16779008 | bytes 2171904 | tf_op jit(solution)/shard_map/dot_general | solution.py:30
  11.8 2.3 %fusion.63 = (f32[256]{0:T(256)S(1)}, f32[8,256]{1,0:T(8,128)S(1)}) fusion(bf16[4,256,4096]{2,1,0:T(8,128)(2,1)} %param.3, bf16[4,8,4096]{2,1,0:T(8,128)(2,1)} %param.4), kind=kOutput, calls=%fused_computation.110 | convolution fusion | flops 16779008 | bytes 2171904 | tf_op jit(solution)/shard_map/dot_general | solution.py:30
  14.1 0.7 slice_bitcast_fusion.3
  14.9 0.1 convert_reduce_fusion.6
  15.0 0.1 convert_reduce_fusion.7
  15.1 0.1 convert_reduce_fusion.4
  15.4 0.1 convert_reduce_fusion
  15.6 0.1 convert_reduce_fusion.2
  15.9 2.3 %fusion.64 = (f32[256]{0:T(256)S(1)}, f32[8,256]{1,0:T(8,128)S(1)}) fusion(bf16[4,256,4096]{2,1,0:T(8,128)(2,1)} %param.3, bf16[4,8,4096]{2,1,0:T(8,128)(2,1)} %param.4), kind=kOutput, calls=%fused_computation.111 | convolution fusion | flops 16779008 | bytes 2171904 | tf_op jit(solution)/shard_map/dot_general | solution.py:30
  18.2 42.0 %all-reduce.1 = (f32[8]{0:T(128)S(1)}, f32[8]{0:T(128)S(1)}, f32[8]{0:T(128)S(1)}, f32[8]{0:T(128)S(1)}) all-reduce(f32[8]{0:T(128)S(1)} %add.50, f32[8]{0:T(128)S(1)} %add.48, f32[8]{0:T(128)S(1)} %add.46, f32[8]{0:T(128)S(1)} %add.44), channel_id=1, replica_groups=mesh['dp'=8,'expert'=4] {'dp','expert'}, use_global_device_ids=true, to_apply=%region_18.0 | all-reduce | flops 32 | bytes 256 | tf_op jit(solution)/shard_map/psum | solution.py:42
  60.2 0.6 multiply_reduce_fusion.6
  60.8 0.7 multiply_reduce_fusion.7
  61.5 0.6 multiply_reduce_fusion.4
  62.1 0.6 multiply_reduce_fusion.5
  62.7 0.2 fusion.55
  62.9 2.0 %convolution_bitcast_fusion.3 = f32[1,8,4096]{2,1,0:T(8,128)S(1)} fusion(bf16[4,256,4096]{2,1,0:T(8,128)(2,1)} %param.3, f32[256]{0:T(256)S(1)} %get-tuple-element.29, f32[256]{0:T(256)S(1)} %get-tuple-element.3, f32[8]{0:T(128)S(1)} %broadcast_multiply_fusion.3, f32[8,256]{1,0:T(8,128)S(1)} %get-tuple-element.43, f32[256]{0:T(256)S(1)} %get-tuple-element.42), kind=kOutput, calls=%fused_computation.3 | convolution fusion | flops 16787456 | bytes 2239520 | tf_op jit(solution)/shard_map/dot_general | solution.py:49
  64.9 2.0 %convolution_bitcast_fusion.2 = f32[1,8,4096]{2,1,0:T(8,128)S(1)} fusion(bf16[4,256,4096]{2,1,0:T(8,128)(2,1)} %param.3, f32[256]{0:T(256)S(1)} %get-tuple-element.31, f32[256]{0:T(256)S(1)} %get-tuple-element.44, f32[8]{0:T(128)S(1)} %broadcast_multiply_fusion.2, f32[8,256]{1,0:T(8,128)S(1)} %get-tuple-element.41, f32[256]{0:T(256)S(1)} %get-tuple-element.40), kind=kOutput, calls=%fused_computation.2 | convolution fusion | flops 16787456 | bytes 2239520 | tf_op jit(solution)/shard_map/dot_general | solution.py:49
  66.9 0.2 fusion.57
  67.1 2.0 %convolution_bitcast_fusion.1 = f32[1,8,4096]{2,1,0:T(8,128)S(1)} fusion(bf16[4,256,4096]{2,1,0:T(8,128)(2,1)} %param.3, f32[256]{0:T(256)S(1)} %get-tuple-element.33, f32[256]{0:T(256)S(1)} %get-tuple-element.7, f32[8]{0:T(128)S(1)} %broadcast_multiply_fusion.1, f32[8,256]{1,0:T(8,128)S(1)} %get-tuple-element.39, f32[256]{0:T(256)S(1)} %get-tuple-element.38), kind=kOutput, calls=%fused_computation.1 | convolution fusion | flops 16787456 | bytes 2239520 | tf_op jit(solution)/shard_map/dot_general | solution.py:49
  69.1 2.0 %convolution_bitcast_fusion = f32[1,8,4096]{2,1,0:T(8,128)S(1)} fusion(bf16[4,256,4096]{2,1,0:T(8,128)(2,1)} %param.3, f32[256]{0:T(256)S(1)} %get-tuple-element.35, f32[256]{0:T(256)S(1)} %get-tuple-element.46, f32[8]{0:T(128)S(1)} %broadcast_multiply_fusion, f32[8,256]{1,0:T(8,128)S(1)} %get-tuple-element.37, f32[256]{0:T(256)S(1)} %get-tuple-element.36), kind=kOutput, calls=%fused_computation | convolution fusion | flops 16787456 | bytes 2239520 | tf_op jit(solution)/shard_map/dot_general | solution.py:49
  71.1 0.8 pad_maximum_fusion
  72.0 2.6 %pad_maximum_fusion.3 = f32[4]{0:T(128)S(1)} fusion(f32[1]{0:T(128)} %bitcast.36, f32[1]{0:T(128)} %bitcast.35, f32[1]{0:T(128)} %bitcast.34, f32[1]{0:T(128)} %bitcast.33), kind=kLoop, calls=%fused_computation.95 | loop fusion | flops 12 | bytes 32 | tf_op jit(solution)/shard_map/stack | solution.py:58
  74.6 40.1 %all-reduce = (f32[4]{0:T(128)S(1)}, f32[4,8]{1,0:T(4,128)S(1)}) all-reduce(f32[4]{0:T(128)S(1)} %pad_maximum_fusion.3, f32[4,8]{1,0:T(4,128)S(1)} %pad_maximum_fusion.1), channel_id=1, replica_groups=mesh['dp'=8,'expert'=4] {'dp','expert'}, use_global_device_ids=true, to_apply=%region_31.0 | all-reduce | flops 36 | bytes 288 | tf_op jit(solution)/shard_map/psum | solution.py:57
  114.6 0.1 fusion.54
  114.8 0.5 collective-permute-start
  115.3 4.0 %collective-permute-done = f32[4,8,512]{2,1,0:T(8,128)S(1)} collective-permute-done((f32[4,8,512]{2,1,0:T(8,128)}, f32[4,8,512]{2,1,0:T(8,128)S(1)}, u32[]{:S(2)}, u32[]{:S(2)}) %collective-permute-start) | collective-permute-done | bytes 65568 | tf_op jit(solution)/shard_map/ppermute | solution.py:54
  119.3 0.9 add.52
  120.2 1.2 collective-permute-start.1
  121.4 0.6 pad_maximum_fusion.2
  121.9 4.1 %collective-permute-done.1 = f32[4,8,512]{2,1,0:T(8,128)S(1)} collective-permute-done((f32[4,8,512]{2,1,0:T(8,128)S(1)}, f32[4,8,512]{2,1,0:T(8,128)S(1)}, u32[]{:S(2)}, u32[]{:S(2)}) %collective-permute-start.1) | collective-permute-done | bytes 65568 | tf_op jit(solution)/shard_map/ppermute | solution.py:54
  126.0 0.6 add.53
  (21 shorter events, 0.5 us)
Async XLA Ops:
  7.2 107.6 %reduce-scatter.2.cloned.1.call-start = ((), (), s32[]{:S(2)}) async-start(), calls=%async_computation.1 | async-start | bytes 589824 | tf_op jit(solution)/shard_map/reduce_scatter | solution.py:51
  114.8 4.5 %collective-permute-start = (f32[4,8,512]{2,1,0:T(8,128)}, f32[4,8,512]{2,1,0:T(8,128)S(1)}, u32[]{:S(2)}, u32[]{:S(2)}) collective-permute-start(f32[4,8,512]{2,1,0:T(8,128)} %reduce-scatter.2.cloned.1.call-done), channel_id=1, source_target_pairs={{0,1},{1,0},{2,3},{3,2},{4,5},{5,4},{6,7},{7,6},{8,9},{9,8},{10,11... | collective-permute-start | bytes 196616 | tf_op jit(solution)/shard_map/ppermute | solution.py:54
  120.2 5.9 %collective-permute-start.1 = (f32[4,8,512]{2,1,0:T(8,128)S(1)}, f32[4,8,512]{2,1,0:T(8,128)S(1)}, u32[]{:S(2)}, u32[]{:S(2)}) collective-permute-start(f32[4,8,512]{2,1,0:T(8,128)S(1)} %add.52), channel_id=1, source_target_pairs={{0,2},{1,3},{2,0},{3,1},{4,6},{5,7},{6,4},{7,5},{8,10},{9,11},{10,... | collective-permute-start | bytes 196616 | tf_op jit(solution)/shard_map/ppermute | solution.py:54
Sparse Core Ops, SparseCore 0:
  72.1 33.9 reduce-scatter.1
